TPU v7x, 8 devices: a whole 2x2x1 slice. The times are simulated.
8 devices in a mesh: dp: 1 (over z), ep: 8 (over y, x, core).
Axes of the slice: x: 2, y: 2, z: 1, core: 2. Of those that a mesh axis runs over, the one named last changes fastest.
Arguments:
- x: bfloat16 [768, 2048], P(('dp', 'ep'))
- route_idx: int32 [768, 6], P(('dp', 'ep'))
- gates: float32 [768, 6], P(('dp', 'ep'))
- w_gate: bfloat16 [64, 2048, 1408], P('ep')
- w_up: bfloat16 [64, 2048, 1408], P('ep')
- w_down: bfloat16 [64, 1408, 2048], P('ep')
- shared_gate: bfloat16 [2048, 2816], replicated
- shared_up: bfloat16 [2048, 2816], replicated
- shared_down: bfloat16 [2816, 2048], replicated
Outputs:
- output: bfloat16 [768, 2048], P(('dp', 'ep'))
All inputs are finite; a program needn't handle non-finite values.
Results may differ from a plain program's by a relative error of at most 0.00804522.
Values are sent between devices in bfloat16 or wider.
A program may use at most 1 GiB of HBM per device.

v0:
```python
import functools

import jax
import jax.numpy as jnp
from jax import lax
from jax.experimental import pallas as pl
from jax.experimental.pallas import tpu as pltpu
from jax.sharding import PartitionSpec as P

MESH = pl.DeviceIdType.MESH
CAP = 36
SLOT = 40
VMEM_LIMIT = 67_000_000
BF16 = jnp.bfloat16
F32 = jnp.float32


def neighbours():
    me = lax.axis_index("ep")
    core = me % 2
    xb = (me // 2) % 2
    yb = me // 4
    sib = me + 1 - 2 * core
    xn = me + 2 - 4 * xb
    yn = me + 4 - 8 * yb
    dg = yn + 2 - 4 * xb
    return me, core, sib, xn, yn, dg


def rcopy(src, dst, send, recv, dev):
    return pltpu.make_async_remote_copy(
        src_ref=src, dst_ref=dst, send_sem=send, recv_sem=recv,
        device_id={"ep": dev}, device_id_type=MESH)


def gather_kernel(x_ref, route_ref, gate_ref, sg_hbm, su_hbm,
                  xall_hbm, hsh_ref, meta_all, cnt_ref, g_ref,
                  land, meta_s, bg, bu, metal,
                  wsem, osem, sx_s, sx_r, sy_s, sy_r, f_s, f_r, ss_s, ss_r, m_s, m_r):
    me, core, sib, xn, yn, dg = neighbours()
    nd = xall_hbm.shape[0]
    rows = x_ref.shape[0]
    half = rows // 2
    n_chunks = bg.shape[0]
    width = bg.shape[2]

    barrier = pltpu.get_barrier_semaphore()
    for r in range(1, nd):
        pl.semaphore_signal(barrier, inc=1, device_id={"ep": (me + r) % nd}, device_id_type=MESH)

    def wcopy(i):
        cols = pl.ds(pl.multiple_of(i * width, width), width)
        return (pltpu.make_async_copy(sg_hbm.at[:, cols], bg.at[i], wsem.at[0, i]),
                pltpu.make_async_copy(su_hbm.at[:, cols], bu.at[i], wsem.at[1, i]))

    for i in range(n_chunks):
        for c in wcopy(i):
            c.start()

    def hs(h):
        return pl.ds(h * half, half)

    own_out = pltpu.make_async_copy(x_ref, xall_hbm.at[me], osem.at[0])
    own_out.start()

    pl.semaphore_wait(barrier, nd - 1)
    own_x = [rcopy(x_ref.at[hs(h)], land.at[me, hs(h)], sx_s.at[h], sx_r.at[h], xn) for h in range(2)]
    own_y = [rcopy(x_ref.at[hs(h)], land.at[me, hs(h)], sy_s.at[h], sy_r.at[h], yn) for h in range(2)]
    own_s = rcopy(x_ref, land.at[me], ss_s.at[0], ss_r.at[0], sib)
    own_x[0].start()
    own_y[1].start()
    own_x[1].start()
    own_y[0].start()
    own_s.start()

    ids = lax.broadcasted_iota(jnp.int32, (rows, 128), 1)
    mask = jnp.zeros((rows, 128), F32)
    gmap = jnp.zeros((rows, 128), F32)
    for k in range(route_ref.shape[1]):
        eq = route_ref[:, k:k + 1] == ids
        mask = mask + jnp.where(eq, 1.0, 0.0)
        gmap = gmap + jnp.where(eq, gate_ref[:, k:k + 1], 0.0)
    lower = (lax.broadcasted_iota(jnp.int32, (rows, rows), 0)
             > lax.broadcasted_iota(jnp.int32, (rows, rows), 1))
    rank = jnp.dot(jnp.where(lower, 1.0, 0.0).astype(BF16), mask.astype(BF16), preferred_element_type=F32)
    rank = jnp.where(mask > 0.0, rank, -1.0)
    count = jnp.broadcast_to(jnp.sum(mask, axis=0, keepdims=True), (8, 128))
    rank_t = jnp.concatenate([rank, jnp.full((128 - rows, 128), -1.0, F32)], axis=0).T
    gate_t = jnp.concatenate([gmap, jnp.zeros((128 - rows, 128), F32)], axis=0).T
    for j in range(nd):
        meta_s[j, 0:8, :] = rank_t[8 * j:8 * j + 8]
        meta_s[j, 8:16, :] = gate_t[8 * j:8 * j + 8]
        meta_s[j, 16:24, :] = count
    metal[me] = meta_s[me]

    def shared_chunk(i):
        for c in wcopy(i):
            c.wait()
        a = jnp.dot(x_ref[...], bg[i], preferred_element_type=F32)
        b = jnp.dot(x_ref[...], bu[i], preferred_element_type=F32)
        cols = pl.ds(pl.multiple_of(i * width, width), width)
        hsh_ref[:, cols] = (jax.nn.silu(a) * b).astype(BF16)

    def shared_range(lo, hi):
        def body(i, carry):
            shared_chunk(i)
            return carry
        lax.fori_loop(lo, hi, body, 0)

    shared_range(0, 1)
    metas = []
    for r in range(1, nd):
        dst = (me + r) % nd
        c = rcopy(meta_s.at[dst], metal.at[me], m_s.at[r - 1], m_r.at[r - 1], dst)
        c.start()
        metas.append(c)

    shared_range(1, n_chunks - 2)

    own_x[0].wait_recv()
    fy = rcopy(land.at[xn, hs(0)], land.at[xn, hs(0)], f_s.at[0], f_r.at[0], yn)
    fy.start()
    sx0 = rcopy(land.at[xn, hs(0)], land.at[xn, hs(0)], ss_s.at[1], ss_r.at[1], sib)
    sx0.start()
    own_y[1].wait_recv()
    fx = rcopy(land.at[yn, hs(1)], land.at[yn, hs(1)], f_s.at[1], f_r.at[1], xn)
    fx.start()
    sy1 = rcopy(land.at[yn, hs(1)], land.at[yn, hs(1)], ss_s.at[2], ss_r.at[2], sib)
    sy1.start()

    shared_range(n_chunks - 2, n_chunks)

    for c in metas:
        c.wait_recv()
    meta_all[...] = metal[...]
    for d in range(nd):
        cnt_ref[d:d + 1, :] = metal[d, 16:17, :].astype(jnp.int32)

    width_g = 8 * SLOT
    lane = lax.broadcasted_iota(jnp.int32, (8, width_g), 1)
    sel = jnp.where(lane // SLOT == lax.broadcasted_iota(jnp.int32, (8, width_g), 0), 1.0, 0.0)
    slot_id = (lax.broadcasted_iota(jnp.int32, (rows, width_g), 1) % SLOT).astype(F32)

    def spread(v):
        return lax.dot_general(v, sel, (((0,), (0,)), ((), ())), preferred_element_type=F32)[:rows]

    def gate_body(d, carry):
        rk = metal[d, 0:8, :]
        gt = metal[d, 8:16, :]
        hi = gt.astype(BF16).astype(F32)
        mid = (gt - hi).astype(BF16).astype(F32)
        lo = gt - hi - mid
        eq = spread(rk) == slot_id
        for q, part in enumerate((hi, mid, lo)):
            g_ref[d, q * rows:(q + 1) * rows, :] = jnp.where(eq, spread(part), 0.0).astype(BF16)
        return carry

    lax.fori_loop(0, nd, gate_body, 0)

    outs = [own_out]

    def emit(d, k):
        c = pltpu.make_async_copy(land.at[d], xall_hbm.at[d], osem.at[k])
        c.start()
        outs.append(c)

    own_s.wait_recv()
    emit(sib, 1)
    own_x[1].wait_recv()
    sx1 = rcopy(land.at[xn, hs(1)], land.at[xn, hs(1)], ss_s.at[3], ss_r.at[3], sib)
    sx1.start()
    emit(xn, 2)
    own_y[0].wait_recv()
    sy0 = rcopy(land.at[yn, hs(0)], land.at[yn, hs(0)], ss_s.at[4], ss_r.at[4], sib)
    sy0.start()
    emit(yn, 3)
    sxn = xn + 1 - 2 * core
    syn = yn + 1 - 2 * core
    sdg = dg + 1 - 2 * core
    sx0.wait_recv()
    sx1.wait_recv()
    emit(sxn, 4)
    sy1.wait_recv()
    sy0.wait_recv()
    emit(syn, 5)
    fy.wait_recv()
    sd0 = rcopy(land.at[dg, hs(0)], land.at[dg, hs(0)], ss_s.at[5], ss_r.at[5], sib)
    sd0.start()
    fx.wait_recv()
    sd1 = rcopy(land.at[dg, hs(1)], land.at[dg, hs(1)], ss_s.at[6], ss_r.at[6], sib)
    sd1.start()
    emit(dg, 6)
    sd0.wait_recv()
    sd1.wait_recv()
    emit(sdg, 7)
    for c in own_x + own_y + [own_s, fy, fx, sx0, sx1, sy0, sy1, sd0, sd1] + metas:
        c.wait_send()
    for c in outs:
        c.wait()


def gather_call(x, route, gates, sg, su, nd):
    rows, d_model = x.shape
    ff = sg.shape[1]
    width = 256
    n_chunks = ff // width
    any_spec = pl.BlockSpec(memory_space=pl.ANY)
    vmem = pl.BlockSpec(memory_space=pltpu.VMEM)
    dma = pltpu.SemaphoreType.DMA
    return pl.pallas_call(
        gather_kernel,
        out_shape=(
            jax.ShapeDtypeStruct((nd, rows, d_model), BF16),
            jax.ShapeDtypeStruct((rows, ff), BF16),
            jax.ShapeDtypeStruct((nd, 24, 128), F32),
            jax.ShapeDtypeStruct((nd, 128), jnp.int32),
            jax.ShapeDtypeStruct((nd, 3 * rows, 8 * SLOT), BF16),
        ),
        in_specs=[vmem, vmem, vmem, any_spec, any_spec],
        out_specs=(any_spec, vmem, vmem, vmem, vmem),
        scratch_shapes=[
            pltpu.VMEM((nd, rows, d_model), BF16),
            pltpu.VMEM((nd, 24, 128), F32),
            pltpu.VMEM((n_chunks, d_model, width), BF16),
            pltpu.VMEM((n_chunks, d_model, width), BF16),
            pltpu.VMEM((nd, 24, 128), F32),
            dma((2, n_chunks)),
            dma((8,)),
            dma((2,)), dma((2,)), dma((2,)), dma((2,)), dma((2,)), dma((2,)),
            dma((7,)), dma((7,)), dma((7,)), dma((7,)),
        ],
        compiler_params=pltpu.CompilerParams(
            collective_id=0, has_side_effects=True, vmem_limit_bytes=VMEM_LIMIT),
        name="gather_shared",
    )(x, route, gates, sg, su)


def hidden_kernel(cnt, meta, xall_hbm, w1_hbm, w3_hbm, h_hbm,
                  xv, wb1, wb3, xg, pos_c, pos_s, hbuf, xsem, wsem, hsem):
    me = lax.axis_index("ep")
    n_exp, d_model, ff = w1_hbm.shape
    nd = meta.shape[0]
    toks = xv.shape[0]
    rows = toks // nd
    depth = wb1.shape[0]
    small = rows
    full = nd * SLOT
    bounds = [(c, min(256, ff - c)) for c in range(0, ff, 256)]

    def wcopy(e, slot, j):
        c0, w = bounds[j]
        return (pltpu.make_async_copy(w1_hbm.at[e, :, c0:c0 + w], wb1.at[slot, :, c0:c0 + w], wsem.at[slot, 0, j]),
                pltpu.make_async_copy(w3_hbm.at[e, :, c0:c0 + w], wb3.at[slot, :, c0:c0 + w], wsem.at[slot, 1, j]))

    xc = pltpu.make_async_copy(xall_hbm, xv, xsem)
    xc.start()
    for e in range(depth):
        for j in range(len(bounds)):
            for c in wcopy(e, e, j):
                c.start()

    row_e = lax.broadcasted_iota(jnp.int32, (8, rows), 0)
    offs = [jnp.int32(0)] * n_exp
    for d in range(nd):
        rk = meta[d, 0:8, 0:rows].astype(jnp.int32)
        off = jnp.zeros((8, rows), jnp.int32)
        for e in range(n_exp):
            off = jnp.where(row_e == e, offs[e], off)
            offs[e] = offs[e] + cnt[d, me * n_exp + e]
        pos_c[:, d * rows:(d + 1) * rows] = jnp.where(rk >= 0, rk + off, -1)
        pos_s[:, d * rows:(d + 1) * rows] = jnp.where(rk >= 0, rk + d * SLOT, -1)
    xc.wait()

    def hcopy(e):
        return pltpu.make_async_copy(hbuf.at[e % 2], h_hbm.at[e], hsem.at[e % 2])

    def gather_rows(pos, m):
        onehot = jnp.where(pos == lax.broadcasted_iota(jnp.int32, (m, toks), 0), 1.0, 0.0).astype(BF16)
        for c0 in range(0, d_model, 512):
            xg[0:m, c0:c0 + 512] = jnp.dot(
                onehot, xv[:, c0:c0 + 512], preferred_element_type=F32).astype(BF16)

    def hidden(slot, j, m):
        c0, w = bounds[j]
        a = jnp.dot(xg[0:m, :], wb1[slot, :, c0:c0 + w], preferred_element_type=F32)
        b = jnp.dot(xg[0:m, :], wb3[slot, :, c0:c0 + w], preferred_element_type=F32)
        return (jax.nn.silu(a) * b).astype(BF16)

    def body(e, carry):
        slot = e % depth
        total = jnp.int32(0)
        for d in range(nd):
            total = total + cnt[d, me * n_exp + e]

        @pl.when(e >= 2)
        def _():
            hcopy(e - 2).wait()

        @pl.when(total <= small)
        def _():
            gather_rows(pos_c[pl.ds(e, 1), :], small)
            slot_row = lax.broadcasted_iota(jnp.int32, (SLOT, small), 0)
            col = lax.broadcasted_iota(jnp.int32, (SLOT, small), 1)
            parts = []
            start = jnp.int32(0)
            for d in range(nd):
                n = cnt[d, me * n_exp + e]
                hit = (col == slot_row + start) & (slot_row < n)
                parts.append(jnp.where(hit, 1.0, 0.0))
                start = start + n
            expand = jnp.concatenate(parts, axis=0).astype(BF16)
            for j, (c0, w) in enumerate(bounds):
                for c in wcopy(e, slot, j):
                    c.wait()
                hid = hidden(slot, j, small)
                hbuf[e % 2, :, c0:c0 + w] = jnp.dot(
                    expand, hid, preferred_element_type=F32).astype(BF16)

        @pl.when(total > small)
        def _():
            gather_rows(pos_s[pl.ds(e, 1), :], full)
            for j, (c0, w) in enumerate(bounds):
                for c in wcopy(e, slot, j):
                    c.wait()
                hbuf[e % 2, :, c0:c0 + w] = hidden(slot, j, full)

        hcopy(e).start()

        @pl.when(e + depth < n_exp)
        def _():
            for j in range(len(bounds)):
                for c in wcopy(e + depth, slot, j):
                    c.start()
        return carry

    lax.fori_loop(0, n_exp, body, 0)
    hcopy(n_exp - 2).wait()
    hcopy(n_exp - 1).wait()


def hidden_call(cnt, meta, xall, w1, w3):
    n_exp, d_model, ff = w1.shape
    toks = xall.shape[0]
    nd = meta.shape[0]
    depth = 3
    any_spec = pl.BlockSpec(memory_space=pl.ANY)
    dma = pltpu.SemaphoreType.DMA
    return pl.pallas_call(
        hidden_kernel,
        out_shape=jax.ShapeDtypeStruct((n_exp, nd * SLOT, ff), BF16),
        in_specs=[pl.BlockSpec(memory_space=pltpu.SMEM), pl.BlockSpec(memory_space=pltpu.VMEM),
                  any_spec, any_spec, any_spec],
        out_specs=any_spec,
        scratch_shapes=[
            pltpu.VMEM((toks, d_model), BF16),
            pltpu.VMEM((depth, d_model, ff), BF16),
            pltpu.VMEM((depth, d_model, ff), BF16),
            pltpu.VMEM((nd * SLOT, d_model), BF16),
            pltpu.VMEM((8, toks), jnp.int32),
            pltpu.VMEM((8, toks), jnp.int32),
            pltpu.VMEM((2, nd * SLOT, ff), BF16),
            dma(()), dma((depth, 2, pl.cdiv(ff, 256))), dma((2,)),
        ],
        compiler_params=pltpu.CompilerParams(vmem_limit_bytes=VMEM_LIMIT),
        name="routed_hidden",
    )(cnt, meta, xall, w1, w3)


def down_kernel(h_hbm, g_hbm, hsh_ref, w2_hbm, sd_hbm, y_ref,
                hv, gv, wb, sdb, ob, snd, kept, in0, in1, in2,
                hsem, gsem, wsem, dsem, s0s, s0r, s1s, s1r, s2s, s2r):
    me, core, sib, xn, yn, dg = neighbours()
    n_exp, full, ff = hv.shape
    nd = gv.shape[0]
    rows = gv.shape[1] // 3
    n_chunks = snd.shape[0]
    width = wb.shape[3]
    depth = wb.shape[0]
    hw = width // 2

    barrier = pltpu.get_barrier_semaphore()
    for dev in (sib, xn, yn):
        pl.semaphore_signal(barrier, inc=1, device_id={"ep": dev}, device_id_type=MESH)

    def wcopy(c, e):
        cols = pl.ds(pl.multiple_of(c * width, width), width)
        slot = c % depth
        return pltpu.make_async_copy(w2_hbm.at[e, :, cols], wb.at[slot, e], wsem.at[slot, e])

    def dcopy(c):
        cols = pl.ds(pl.multiple_of(c * width, width), width)
        return pltpu.make_async_copy(sd_hbm.at[:, cols], sdb.at[c], dsem.at[c])

    def hcopy(e):
        return pltpu.make_async_copy(h_hbm.at[e], hv.at[e], hsem.at[e])

    gcopy = pltpu.make_async_copy(g_hbm, gv, gsem)
    for e in range(n_exp):
        hcopy(e).start()
        wcopy(0, e).start()
    gcopy.start()
    for c in range(1, depth):
        for e in range(n_exp):
            wcopy(c, e).start()

    own_c, xn_c, yn_c, dg_c = me // 2, xn // 2, yn // 2, dg // 2
    orders = ((own_c, yn_c, xn_c, dg_c), (own_c, xn_c, yn_c, dg_c))
    first_hop = (xn, yn)
    second_hop = (yn, xn)

    def send0(c):
        return rcopy(snd.at[c], in0.at[c], s0s.at[c], s0r.at[c], sib)

    def send1(c, q):
        return rcopy(kept.at[c, q, pl.ds(2, 2)], in1.at[c, q], s1s.at[c, q], s1r.at[c, q], first_hop[q])

    def send2(c, q):
        return rcopy(kept.at[c, q, 1], in2.at[c, q], s2s.at[c, q], s2r.at[c, q], second_hop[q])

    def step0(c):
        send0(c).wait_recv()
        kept[c] = kept[c] + in0[c]

    def step1(c):
        for q in range(2):
            send1(c, q).wait_recv()
            kept[c, q, 0:2] = kept[c, q, 0:2] + in1[c, q]

    def step2(c):
        for q in range(2):
            send2(c, q).wait_recv()
            kept[c, q, 0] = kept[c, q, 0] + in2[c, q]

    def start1(c):
        send1(c, 0).start()
        send1(c, 1).start()

    def start2(c):
        send2(c, 0).start()
        send2(c, 1).start()

    def expert(c, e):
        wcopy(c, e).wait()
        out = jnp.dot(hv[e], wb[c % depth, e], preferred_element_type=F32)
        out = out.astype(BF16).astype(F32)
        ob[:, e] = out.reshape(nd, SLOT, width)

    def gated(d):
        o = ob[d].reshape(n_exp * SLOT, width).astype(BF16)
        r = jnp.dot(gv[d], o, preferred_element_type=F32)
        return r[0:rows] + r[rows:2 * rows] + r[2 * rows:3 * rows]

    def chunk(c, carry):
        for e in range(n_exp):
            @pl.when(c == 0)
            def _():
                hcopy(e).wait()
            expert(c, e)

            @pl.when(c + depth < n_chunks)
            def _():
                wcopy(c + depth, e).start()

            if e == n_exp // 2 - 1:
                @pl.when(c >= 1)
                def _():
                    step0(c - 1)

                @pl.when(c >= 2)
                def _():
                    step1(c - 2)

                @pl.when(c >= 1)
                def _():
                    start1(c - 1)

                @pl.when(c >= 2)
                def _():
                    start2(c - 2)

        dcopy(c).start()

        @pl.when(c == 0)
        def _():
            gcopy.wait()
        chips = (own_c, xn_c, yn_c, dg_c)
        where = ((0, 0), (2, 1), (1, 2), (3, 3))
        for chip, (p0, p1) in zip(chips, where):
            r = gated(2 * chip + 1 - core)
            snd[c, 0, p0] = r[:, 0:hw]
            snd[c, 1, p1] = r[:, hw:width]
        for chip, (p0, p1) in zip(chips, where):
            r = gated(2 * chip + core)
            kept[c, 0, p0] = r[:, 0:hw]
            kept[c, 1, p1] = r[:, hw:width]

        send0(c).start()
        return carry

    pl.semaphore_wait(barrier, 3)
    lax.fori_loop(0, n_chunks, chunk, 0)

    def shared(c):
        dcopy(c).wait()
        cols = pl.ds(pl.multiple_of(c * width, width), width)
        s = jnp.dot(hsh_ref[...], sdb[c], preferred_element_type=F32).astype(BF16)
        y_ref[:, cols] = s

    def shared_range(lo, hi):
        def body(c, carry):
            shared(c)
            return carry
        lax.fori_loop(lo, hi, body, 0)

    last = n_chunks - 1
    shared_range(0, 3)
    step0(last)
    step1(last - 1)
    start1(last)
    start2(last - 1)
    shared_range(3, n_chunks)
    step1(last)
    start2(last)

    def finish(c, carry):
        step2(c)
        for q in range(2):
            cols = pl.ds(pl.multiple_of(c * width + q * hw, hw), hw)
            y_ref[:, cols] = (y_ref[:, cols].astype(F32) + kept[c, q, 0]).astype(BF16)
        return carry

    lax.fori_loop(0, n_chunks, finish, 0)

    def drain(c, carry):
        send0(c).wait_send()
        for q in range(2):
            send1(c, q).wait_send()
            send2(c, q).wait_send()
        return carry

    lax.fori_loop(0, n_chunks, drain, 0)


def down_call(h, g, hsh, w2, sd):
    n_exp, full, ff = h.shape
    nd, rows3, width_g = g.shape
    rows = rows3 // 3
    d_model = w2.shape[2]
    width = 256
    n_chunks = d_model // width
    depth = 3
    hw = width // 2
    any_spec = pl.BlockSpec(memory_space=pl.ANY)
    vmem = pl.BlockSpec(memory_space=pltpu.VMEM)
    dma = pltpu.SemaphoreType.DMA
    return pl.pallas_call(
        down_kernel,
        out_shape=jax.ShapeDtypeStruct((rows, d_model), BF16),
        in_specs=[any_spec, any_spec, vmem, any_spec, any_spec],
        out_specs=vmem,
        scratch_shapes=[
            pltpu.VMEM((n_exp, full, ff), BF16),
            pltpu.VMEM((nd, rows3, width_g), BF16),
            pltpu.VMEM((depth, n_exp, ff, width), BF16),
            pltpu.VMEM((n_chunks, sd.shape[0], width), BF16),
            pltpu.VMEM((nd, n_exp, SLOT, width), F32),
            pltpu.VMEM((n_chunks, 2, 4, rows, hw), F32),
            pltpu.VMEM((n_chunks, 2, 4, rows, hw), F32),
            pltpu.VMEM((n_chunks, 2, 4, rows, hw), F32),
            pltpu.VMEM((n_chunks, 2, 2, rows, hw), F32),
            pltpu.VMEM((n_chunks, 2, rows, hw), F32),
            dma((n_exp,)), dma(()), dma((depth, n_exp)), dma((n_chunks,)),
            dma((n_chunks,)), dma((n_chunks,)),
            dma((n_chunks, 2)), dma((n_chunks, 2)), dma((n_chunks, 2)), dma((n_chunks, 2)),
        ],
        compiler_params=pltpu.CompilerParams(
            collective_id=1, has_side_effects=True, vmem_limit_bytes=VMEM_LIMIT),
        name="down_reduce",
    )(h, g, hsh, w2, sd)


def solution(mesh):
    nd = mesh.shape["ep"]

    def device_fn(x, route, gates, w_gate, w_up, w_down, sg, su, sd):
        xall, hsh, meta, cnt, g = gather_call(x, route, gates, sg, su, nd)
        h = hidden_call(cnt, meta, xall.reshape(nd * x.shape[0], x.shape[1]), w_gate, w_up)
        return down_call(h, g, hsh, w_down, sd)

    tok = P(("dp", "ep"), None)
    exp = P("ep", None, None)
    rep = P(None, None)
    return jax.shard_map(device_fn, mesh=mesh, in_specs=(tok, tok, tok, exp, exp, exp, rep, rep, rep),
                         out_specs=tok, check_vma=False)
```

profile of v0, /device:TPU:0, one launch (start us, length us, event | category | flops | bytes accessed | tf_op | source)
XLA Modules:
  0.0 150.0 jit_solution(15252419986628034942)
XLA Ops:
  0.0 1.4 copy.10.route_ref
  1.4 1.4 copy.11.gate_ref
  2.8 24.8 %gather_shared.1 = (bf16[8,96,2048]{2,1,0:T(8,128)(2,1)}, bf16[96,2816]{1,0:T(8,128)(2,1)}, f32[8,24,128]{2,1,0:T(8,128)}, s32[8,128]{1,0:T(8,128)}, bf16[8,288,320]{2,1,0:T(8,128)(2,1)}) custom-call(bf16[96,2048]{1,0:T(8,128)(2,1)} %x_ref.1, s32[96,6]{1,0:T(8,128)} %copy.10.route_ref, f32[96,6]{1,0:T(8,128)} %copy.11.gate_ref, bf16[2048,2816]{1,0:T(8,128)(2,1)} %sg_hbm.1, ...), custom_call_target="tpu_custom_call" | custom-call | tf_op jit(solution)/shard_map/gather_shared/pallas_call | solution.py:210
  27.6 53.8 %routed_hidden.1.h_hbm = bf16[8,320,1408]{2,1,0:T(8,128)(2,1)} custom-call(s32[8,128]{1,0:T(8,128)} %get-tuple-element.10.cnt, f32[8,24,128]{2,1,0:T(8,128)} %get-tuple-element.11.meta, bf16[768,2048]{1,0:T(8,128)(2,1)} %bitcast.1, bf16[8,2048,1408]{2,1,0:T(8,128)(2,1)} %w1_hbm.1, bf16[8,2048,1408]{2,1,0:T(8,128)(2,1)} %w3_hbm.1), custom_call_target="tpu_custom_call" | custom-call | tf_op jit(solution)/shard_map/routed_hidden/pallas_call | solution.py:348
  81.5 66.8 %down_reduce.1 = bf16[96,2048]{1,0:T(8,128)(2,1)} custom-call(bf16[8,320,1408]{2,1,0:T(8,128)(2,1)} %routed_hidden.1.h_hbm, bf16[8,288,320]{2,1,0:T(8,128)(2,1)} %get-tuple-element.13.g_hbm, bf16[96,2816]{1,0:T(8,128)(2,1)} %get-tuple-element.14.hsh_ref, bf16[8,1408,2048]{2,1,0:T(8,128)(2,1)} %w2_hbm.1, bf16[2816,2048]{1,0:T(8,128)(2,1)} %sd_hbm.1), custom_call_target="tpu_custom_call" | custom-call | tf_op jit(solution)/shard_map/down_reduce/pallas_call | solution.py:556
  148.2 1.8 %copy.13 = bf16[96,2048]{1,0:T(8,128)(2,1)} copy(bf16[96,2048]{1,0:T(8,128)(2,1)} %down_reduce.1) | data formatting | bytes 786432
where the time goes:
time: 150 us
  Pallas kernels  145 us (97%)
  local copies, waits for them, and re-layouts  4.57 us (3%)
    pallas_call x1, Pallas kernels, down_call(): pl.pallas_call(down_kernel, out_shape=jax.ShapeDtypeStruct((rows, d_model...  66.8 us
    pallas_call x1, Pallas kernels, hidden_call(): pl.pallas_call(hidden_kernel, out_shape=jax.ShapeDtypeStruct((n_exp, nd *...  53.8 us
    pallas_call x1, Pallas kernels, gather_call(): pl.pallas_call(gather_kernel, out_shape=(jax.ShapeDtypeStruct((nd, rows,...  24.8 us
    unnamed x3, local copies, waits for them, and re-layouts  4.57 us

commit v1 on v0

--- a/solution.py
+++ b/solution.py
@@ -246,16 +246,18 @@
     small = rows
     full = nd * SLOT
     bounds = [(c, min(256, ff - c)) for c in range(0, ff, 256)]
+    cut = 3 * 256
+    groups = ((0, cut, bounds[:3]), (cut, ff - cut, bounds[3:]))
 
     def wcopy(e, slot, j):
-        c0, w = bounds[j]
+        c0, w, _ = groups[j]
         return (pltpu.make_async_copy(w1_hbm.at[e, :, c0:c0 + w], wb1.at[slot, :, c0:c0 + w], wsem.at[slot, 0, j]),
                 pltpu.make_async_copy(w3_hbm.at[e, :, c0:c0 + w], wb3.at[slot, :, c0:c0 + w], wsem.at[slot, 1, j]))
 
     xc = pltpu.make_async_copy(xall_hbm, xv, xsem)
     xc.start()
     for e in range(depth):
-        for j in range(len(bounds)):
+        for j in range(len(groups)):
             for c in wcopy(e, e, j):
                 c.start()
 
@@ -280,8 +282,7 @@
             xg[0:m, c0:c0 + 512] = jnp.dot(
                 onehot, xv[:, c0:c0 + 512], preferred_element_type=F32).astype(BF16)
 
-    def hidden(slot, j, m):
-        c0, w = bounds[j]
+    def hidden(slot, c0, w, m):
         a = jnp.dot(xg[0:m, :], wb1[slot, :, c0:c0 + w], preferred_element_type=F32)
         b = jnp.dot(xg[0:m, :], wb3[slot, :, c0:c0 + w], preferred_element_type=F32)
         return (jax.nn.silu(a) * b).astype(BF16)
@@ -309,26 +310,28 @@
                 parts.append(jnp.where(hit, 1.0, 0.0))
                 start = start + n
             expand = jnp.concatenate(parts, axis=0).astype(BF16)
-            for j, (c0, w) in enumerate(bounds):
+            for j, (_, _, cols) in enumerate(groups):
                 for c in wcopy(e, slot, j):
                     c.wait()
-                hid = hidden(slot, j, small)
-                hbuf[e % 2, :, c0:c0 + w] = jnp.dot(
-                    expand, hid, preferred_element_type=F32).astype(BF16)
+                for c0, w in cols:
+                    hid = hidden(slot, c0, w, small)
+                    hbuf[e % 2, :, c0:c0 + w] = jnp.dot(
+                        expand, hid, preferred_element_type=F32).astype(BF16)
 
         @pl.when(total > small)
         def _():
             gather_rows(pos_s[pl.ds(e, 1), :], full)
-            for j, (c0, w) in enumerate(bounds):
+            for j, (_, _, cols) in enumerate(groups):
                 for c in wcopy(e, slot, j):
                     c.wait()
-                hbuf[e % 2, :, c0:c0 + w] = hidden(slot, j, full)
+                for c0, w in cols:
+                    hbuf[e % 2, :, c0:c0 + w] = hidden(slot, c0, w, full)
 
         hcopy(e).start()
 
         @pl.when(e + depth < n_exp)
         def _():
-            for j in range(len(bounds)):
+            for j in range(len(groups)):
                 for c in wcopy(e + depth, slot, j):
                     c.start()
         return carry
@@ -359,7 +362,7 @@
             pltpu.VMEM((8, toks), jnp.int32),
             pltpu.VMEM((8, toks), jnp.int32),
             pltpu.VMEM((2, nd * SLOT, ff), BF16),
-            dma(()), dma((depth, 2, pl.cdiv(ff, 256))), dma((2,)),
+            dma(()), dma((depth, 2, 2)), dma((2,)),
         ],
         compiler_params=pltpu.CompilerParams(vmem_limit_bytes=VMEM_LIMIT),
         name="routed_hidden",
@@ -440,7 +443,6 @@
         send2(c, 1).start()
 
     def expert(c, e):
-        wcopy(c, e).wait()
         out = jnp.dot(hv[e], wb[c % depth, e], preferred_element_type=F32)
         out = out.astype(BF16).astype(F32)
         ob[:, e] = out.reshape(nd, SLOT, width)
@@ -451,17 +453,22 @@
         return r[0:rows] + r[rows:2 * rows] + r[2 * rows:3 * rows]
 
     def chunk(c, carry):
-        for e in range(n_exp):
+        for e0 in range(0, n_exp, 4):
             @pl.when(c == 0)
             def _():
-                hcopy(e).wait()
-            expert(c, e)
+                for e in range(e0, e0 + 4):
+                    hcopy(e).wait()
+            for e in range(e0, e0 + 4):
+                wcopy(c, e).wait()
+            for e in range(e0, e0 + 4):
+                expert(c, e)
 
             @pl.when(c + depth < n_chunks)
             def _():
-                wcopy(c + depth, e).start()
-
-            if e == n_exp // 2 - 1:
+                for e in range(e0, e0 + 4):
+                    wcopy(c + depth, e).start()
+
+            if e0 == 0:
                 @pl.when(c >= 1)
                 def _():
                     step0(c - 1)

time: 150 us -> 128 us (0.85)
  Pallas kernels: 145 us -> 124 us
    pallas_call x1, Pallas kernels: 66.8 us -> 52.9 us  [down_call(): pl.pallas_call(down_kernel, out_shape=jax.ShapeDtypeStruct((rows, d_model...]
    pallas_call x1, Pallas kernels: 53.8 us -> 46.5 us  [hidden_call(): pl.pallas_call(hidden_kernel, out_shape=jax.ShapeDtypeStruct((n_exp, nd *...]
where the time goes in v1:
time: 128 us; the launch traced here: 129 us
  Pallas kernels  124 us (97%)
  local copies, waits for them, and re-layouts  4.57 us (4%)
    pallas_call x1, Pallas kernels, down_call(): pl.pallas_call(down_kernel, out_shape=jax.ShapeDtypeStruct((rows, d_model...  52.9 us
    pallas_call x1, Pallas kernels, hidden_call(): pl.pallas_call(hidden_kernel, out_shape=jax.ShapeDtypeStruct((n_exp, nd *...  46.5 us
    pallas_call x1, Pallas kernels, gather_call(): pl.pallas_call(gather_kernel, out_shape=(jax.ShapeDtypeStruct((nd, rows,...  24.8 us
    unnamed x3, local copies, waits for them, and re-layouts  4.57 us

profile of v1, /device:TPU:0, one launch (start us, length us, event | category | flops | bytes accessed | tf_op | source)
XLA Modules:
  0.0 128.7 jit_solution(11837736825747850367)
XLA Ops:
  0.0 1.4 %copy.10.route_ref = s32[96,6]{1,0:T(8,128)} copy(s32[96,6]{0,1:T(8,128)} %param.10) | data formatting | bytes 4608 | tf_op args[1]
  1.4 1.4 %copy.11.gate_ref = f32[96,6]{1,0:T(8,128)} copy(f32[96,6]{0,1:T(8,128)} %param.11) | data formatting | bytes 4608 | tf_op args[2]
  2.8 24.8 %gather_shared.1 = (bf16[8,96,2048]{2,1,0:T(8,128)(2,1)}, bf16[96,2816]{1,0:T(8,128)(2,1)}, f32[8,24,128]{2,1,0:T(8,128)}, s32[8,128]{1,0:T(8,128)}, bf16[8,288,320]{2,1,0:T(8,128)(2,1)}) custom-call(bf16[96,2048]{1,0:T(8,128)(2,1)} %x_ref.1, s32[96,6]{1,0:T(8,128)} %copy.10.route_ref, f32[96,6]{1,0:T(8,128)} %copy.11.gate_ref, bf16[2048,2816]{1,0:T(8,128)(2,1)} %sg_hbm.1, ...), custom_call_target="tpu_custom_call" | custom-call | tf_op jit(solution)/shard_map/gather_shared/pallas_call | solution.py:210
  27.6 46.5 %routed_hidden.1.h_hbm = bf16[8,320,1408]{2,1,0:T(8,128)(2,1)} custom-call(s32[8,128]{1,0:T(8,128)} %get-tuple-element.10.cnt, f32[8,24,128]{2,1,0:T(8,128)} %get-tuple-element.11.meta, bf16[768,2048]{1,0:T(8,128)(2,1)} %bitcast.1, bf16[8,2048,1408]{2,1,0:T(8,128)(2,1)} %w1_hbm.1, bf16[8,2048,1408]{2,1,0:T(8,128)(2,1)} %w3_hbm.1), custom_call_target="tpu_custom_call" | custom-call | tf_op jit(solution)/shard_map/routed_hidden/pallas_call | solution.py:351
  74.1 52.9 %down_reduce.1 = bf16[96,2048]{1,0:T(8,128)(2,1)} custom-call(bf16[8,320,1408]{2,1,0:T(8,128)(2,1)} %routed_hidden.1.h_hbm, bf16[8,288,320]{2,1,0:T(8,128)(2,1)} %get-tuple-element.13.g_hbm, bf16[96,2816]{1,0:T(8,128)(2,1)} %get-tuple-element.14.hsh_ref, bf16[8,1408,2048]{2,1,0:T(8,128)(2,1)} %w2_hbm.1, bf16[2816,2048]{1,0:T(8,128)(2,1)} %sd_hbm.1), custom_call_target="tpu_custom_call" | custom-call | tf_op jit(solution)/shard_map/down_reduce/pallas_call | solution.py:563
  127.0 1.8 %copy.13 = bf16[96,2048]{1,0:T(8,128)(2,1)} copy(bf16[96,2048]{1,0:T(8,128)(2,1)} %down_reduce.1) | data formatting | bytes 786432
